TPU v7x, 32 devices: a whole 2x2x4 slice. The times are simulated.
32 devices in a mesh: groups: 2 (over y), seq: 4 (over z), tensor: 4 (over x, core).
Axes of the slice: x: 2, y: 2, z: 4, core: 2. Of those that a mesh axis runs over, the one named last changes fastest.
Arguments:
- final_block_queries: bfloat16 [256, 8192], P(('groups', 'seq'), 'tensor'), parts along dimension 0, may hold values from -96 to 96
- final_block_keys: bfloat16 [256, 1024], P(('groups', 'seq'), 'tensor'), parts along dimension 0, may hold values from -16 to 16
- final_block_values: bfloat16 [256, 1024], P(('groups', 'seq'), 'tensor'), parts along dimension 0, may hold values from -6 to 6
- prompt_cached_keys: bfloat16 [12288, 1024], P(('groups', 'seq'), 'tensor'), parts along dimension 0, may hold values from -16 to 16
- prompt_cached_values: bfloat16 [12288, 1024], P(('groups', 'seq'), 'tensor'), parts along dimension 0, may hold values from -6 to 6
- paged_cache_pool: bfloat16 [256, 128, 2, 1024], P(('groups', 'seq'), None, None, 'tensor'), parts along dimension 0, may hold values from -16 to 16
- step_slot_queries: bfloat16 [32, 4, 8192], P(('groups', 'seq'), None, 'tensor'), parts along dimension 0, may hold values from -96 to 96
- step_token_keys: bfloat16 [32, 4, 1024], P(('groups', 'seq'), None, 'tensor'), parts along dimension 0, may hold values from -16 to 16
- step_token_values: bfloat16 [32, 4, 1024], P(('groups', 'seq'), None, 'tensor'), parts along dimension 0, may hold values from -6 to 6
- normed_step_inputs: bfloat16 [32, 4, 8192], P(('groups', 'seq'), None, 'tensor'), parts along dimension 0, may hold values from -6 to 6
- adapter_down_maps: bfloat16 [8192, 128], P('tensor'), may hold values from -0.0625 to 0.0625
- adapter_up_maps: bfloat16 [128, 8192], P(None, 'tensor'), may hold values from -1.5 to 1.5
- slot_request: int32 [32], P('groups'), parts along dimension 0, may hold values from 0 to 15, as said below
- request_page_table: int32 [32, 8], P('groups'), parts along dimension 0, may hold values from 0 to 127, as said below
- lengths: int32 [32], P('groups'), parts along dimension 0, may hold values from 2 to 1024, as said below
- request_adapter: int32 [32], P('groups'), parts along dimension 0, may hold values from 0 to 7
- request_rank: int32 [32], P('groups'), parts along dimension 0, may hold values from 4 to 16
Outputs:
- prefill_out: bfloat16 [256, 8192], P(('groups', 'seq'), 'tensor'), parts along dimension 0
- decode_out: bfloat16 [32, 4, 8192], P(('groups', 'seq'), None, 'tensor'), parts along dimension 0
There are 2 independent parts, one for each index of `groups`. A program takes and returns all parts, laid end to end along the dimension named above; an argument that names none is the same for every part. Nothing has to cross between parts.
Inputs may be any that keep to these rules, and one draw needn't show every extreme that they name: A permutation: slot k serves request slot_request[k]; the owner of slots k * 4 to (k + 1) * 4 - 1 is owner k. `request_page_table`: every pool page is named exactly once. For every owner and every block of 32 pool pages (pages b * 32 to (b + 1) * 32 - 1), exactly 8 of the pages of that owner's requests lie in the block. `lengths`: some request has exactly 1024 cached tokens.
All inputs are finite; a program needn't handle non-finite values.
Results may differ from a plain program's by a relative error of at most 0.028.
Values may be sent and summed in bfloat16 or wider, within the bound.
No kernel may reach another device: no remote copies, remote signals or barrier semaphores. Data moves between devices by JAX's collectives and lax.ppermute only.
A program may use at most 128 MiB of HBM per device.

v0:
```python
import jax
import jax.numpy as jnp
from jax import lax
from jax.sharding import PartitionSpec as P

HEAD_SIZE = 128
LARGEST_RANK = 16
MASKED = -1e30


def lookup_rows(lookup, positions):
    hit_mask = positions[..., None] == jnp.arange(lookup.shape[0], dtype=jnp.int32)
    if lookup.ndim == 1:
        return jnp.sum(jnp.where(hit_mask, lookup, 0), axis=-1)
    return jnp.sum(jnp.where(hit_mask[..., None], lookup, 0), axis=-2)


def partial_softmax(query_vectors, paged_key_rows, paged_value_rows, allowed):
    batch_count, query_total_count, query_width = query_vectors.shape
    kv_heads = paged_key_rows.shape[2] // HEAD_SIZE
    heads_per_group = query_width // HEAD_SIZE // kv_heads
    query_head_rows = query_vectors.reshape(
        batch_count, query_total_count, kv_heads, heads_per_group, HEAD_SIZE
    )
    key_head_rows = paged_key_rows.reshape(
        batch_count, paged_key_rows.shape[1], kv_heads, HEAD_SIZE
    )
    value_head_rows = paged_value_rows.reshape(
        batch_count, paged_value_rows.shape[1], kv_heads, HEAD_SIZE
    )
    scores = jnp.einsum(
        "etkgd,epkd->ekgtp", query_head_rows, key_head_rows, preferred_element_type=jnp.float32
    ) * HEAD_SIZE ** (-0.5)
    key_mask = allowed[:, None, None, :, :]
    scores = jnp.where(key_mask, scores, MASKED)
    row_max = jnp.max(scores, axis=-1)
    weights = jnp.where(key_mask, jnp.exp(scores - row_max[..., None]), 0.0)
    row_total = jnp.sum(weights, axis=-1)
    summed = jnp.einsum(
        "ekgtp,epkd->etkgd",
        weights.astype(jnp.bfloat16),
        value_head_rows,
        preferred_element_type=jnp.float32,
    )
    heads_here = kv_heads * heads_per_group
    row_max = jnp.transpose(row_max, (0, 3, 1, 2)).reshape(
        batch_count, query_total_count, heads_here
    )
    row_total = jnp.transpose(row_total, (0, 3, 1, 2)).reshape(
        batch_count, query_total_count, heads_here
    )
    return (
        summed.reshape(batch_count, query_total_count, heads_here, HEAD_SIZE),
        row_max,
        row_total,
    )


def combine(summed, row_max, row_total, along):
    best_max = jnp.max(row_max, axis=along, keepdims=True)
    factor = jnp.exp(row_max - best_max)
    whole_total = jnp.sum(factor * row_total, axis=along)
    merged = jnp.sum(factor[..., None] * summed, axis=along)
    return merged / whole_total[..., None]


def per_device(
    final_block_queries,
    final_block_keys,
    final_block_values,
    prompt_cached_keys,
    prompt_cached_values,
    paged_cache_pool,
    step_slot_queries,
    step_token_keys,
    step_token_values,
    normed_step_inputs,
    adapter_down_maps,
    adapter_up_maps,
    slot_request,
    request_page_table,
    lengths,
    request_adapter,
    request_rank,
):
    seq_count = lax.axis_size("seq")
    position = lax.axis_index("seq")
    span_rows = final_block_queries.shape[0]
    ctx_rows = prompt_cached_keys.shape[0]
    heads_here = final_block_queries.shape[1] // HEAD_SIZE
    everyone = lax.all_gather(final_block_queries, "seq", axis=0, tiled=True)
    span_total = everyone.shape[0]
    block_rows = min(128, span_total)
    paged_key_rows = jnp.concatenate([prompt_cached_keys, final_block_keys], axis=0)
    paged_value_rows = jnp.concatenate([prompt_cached_values, final_block_values], axis=0)
    spots = jnp.arange(paged_key_rows.shape[0], dtype=jnp.int32)
    key_pos = jnp.where(spots < ctx_rows, -1, position * span_rows + spots - ctx_rows)

    def run_block(row_start):
        query_rows = lax.dynamic_slice_in_dim(everyone, row_start, block_rows, 0)
        row_pos = row_start + jnp.arange(block_rows, dtype=jnp.int32)
        allowed = key_pos[None, :] <= row_pos[:, None]
        summed, row_max, row_total = partial_softmax(
            query_rows[None], paged_key_rows[None], paged_value_rows[None], allowed[None]
        )
        return (summed[0], row_max[0], row_total[0])

    starts = jnp.arange(span_total // block_rows, dtype=jnp.int32) * block_rows
    summed, row_max, row_total = lax.map(run_block, starts)
    summed = summed.reshape(span_total, heads_here, HEAD_SIZE)
    row_max = row_max.reshape(span_total, heads_here)
    row_total = row_total.reshape(span_total, heads_here)
    returned = (
        lax.all_to_all(summed, "seq", split_axis=0, concat_axis=0, tiled=True),
        lax.all_to_all(row_max, "seq", split_axis=0, concat_axis=0, tiled=True),
        lax.all_to_all(row_total, "seq", split_axis=0, concat_axis=0, tiled=True),
    )
    block_sums = returned[0].reshape(seq_count, span_rows, heads_here, HEAD_SIZE)
    block_maxes = returned[1].reshape(seq_count, span_rows, heads_here)
    block_totals = returned[2].reshape(seq_count, span_rows, heads_here)
    prefill_out = (
        combine(block_sums, block_maxes, block_totals, 0)
        .reshape(span_rows, heads_here * HEAD_SIZE)
        .astype(jnp.bfloat16)
    )
    slots_total = slot_request.shape[0]
    slots_here = slots_total // seq_count
    page_count = request_page_table.shape[1]
    pool_here = paged_cache_pool.shape[0]
    page_len = paged_cache_pool.shape[1]
    per_owner = slots_here * page_count // seq_count
    entries = slots_here * page_count
    decode_step_count = step_slot_queries.shape[1]
    slot_page_list = lookup_rows(request_page_table, slot_request)
    slot_length = lookup_rows(lengths, slot_request)
    owner_pages = slot_page_list.reshape(seq_count, entries)
    holder = owner_pages // pool_here
    pool_place = owner_pages % pool_here
    is_mine = holder == position
    rank_in = jnp.cumsum(is_mine.astype(jnp.int32), axis=1) - 1
    hit_mask = is_mine[:, :, None] & (rank_in[:, :, None] == jnp.arange(per_owner, dtype=jnp.int32))
    send_place = jnp.sum(jnp.where(hit_mask, pool_place[:, :, None], 0), axis=1).reshape(-1)
    entry_ids = jnp.arange(entries, dtype=jnp.int32)
    outgoing = paged_cache_pool[send_place]
    my_holder = lax.dynamic_index_in_dim(holder, position, 0, keepdims=False)
    before = (my_holder[None, :] == my_holder[:, None]) & (entry_ids[None, :] < entry_ids[:, None])
    arrive = my_holder * per_owner + jnp.sum(before.astype(jnp.int32), axis=1)
    my_requests = lax.dynamic_slice_in_dim(slot_request, position * slots_here, slots_here)
    my_lengths = lax.dynamic_slice_in_dim(slot_length, position * slots_here, slots_here)
    adapters = lookup_rows(request_adapter, my_requests)
    ranks = lookup_rows(request_rank, my_requests)
    hidden_input_rows = normed_step_inputs.reshape(
        slots_here * decode_step_count, normed_step_inputs.shape[2]
    )
    reduced_rank_state = lax.psum(
        jnp.dot(hidden_input_rows, adapter_down_maps, preferred_element_type=jnp.float32), "tensor"
    )
    column_indices = jnp.arange(adapter_down_maps.shape[1], dtype=jnp.int32)
    rank_keep_mask = (column_indices[None, :] // LARGEST_RANK == adapters[:, None]) & (
        column_indices[None, :] % LARGEST_RANK < ranks[:, None]
    )
    adapter_kept_rank = jnp.where(
        jnp.repeat(rank_keep_mask, decode_step_count, axis=0), reduced_rank_state, 0.0
    ).astype(jnp.bfloat16)
    raised_queries = jnp.dot(
        adapter_kept_rank, adapter_up_maps, preferred_element_type=jnp.float32
    ).reshape(slots_here, decode_step_count, -1)
    query_vectors = (step_slot_queries.astype(jnp.float32) + raised_queries).astype(jnp.bfloat16)
    step_pos = jnp.arange(decode_step_count, dtype=jnp.int32)
    fresh_ok = step_pos[None, :] <= step_pos[:, None]
    incoming = lax.all_to_all(outgoing, "seq", split_axis=0, concat_axis=0, tiled=True)
    gathered_pages = incoming[arrive].reshape(slots_here, page_count * page_len, 2, -1)
    all_keys = jnp.concatenate([gathered_pages[:, :, 0], step_token_keys], axis=1)
    all_values = jnp.concatenate([gathered_pages[:, :, 1], step_token_values], axis=1)
    cache_pos = jnp.arange(page_count * page_len, dtype=jnp.int32)
    cache_ok = jnp.broadcast_to(
        cache_pos[None, None, :] < my_lengths[:, None, None],
        (slots_here, decode_step_count, page_count * page_len),
    )
    allowed = jnp.concatenate(
        [
            cache_ok,
            jnp.broadcast_to(fresh_ok[None], (slots_here, decode_step_count, decode_step_count)),
        ],
        axis=2,
    )
    summed, row_max, row_total = partial_softmax(query_vectors, all_keys, all_values, allowed)
    decode_out = (
        (summed / row_total[..., None])
        .reshape(slots_here, decode_step_count, -1)
        .astype(jnp.bfloat16)
    )
    return (prefill_out, decode_out)


def solution(mesh):
    placed = (
        P(("groups", "seq"), "tensor"),
        P(("groups", "seq"), "tensor"),
        P(("groups", "seq"), "tensor"),
        P(("groups", "seq"), "tensor"),
        P(("groups", "seq"), "tensor"),
        P(("groups", "seq"), None, None, "tensor"),
        P(("groups", "seq"), None, "tensor"),
        P(("groups", "seq"), None, "tensor"),
        P(("groups", "seq"), None, "tensor"),
        P(("groups", "seq"), None, "tensor"),
        P("tensor", None),
        P(None, "tensor"),
        P("groups"),
        P("groups", None),
        P("groups"),
        P("groups"),
        P("groups"),
    )
    return jax.shard_map(
        per_device,
        mesh=mesh,
        in_specs=placed,
        out_specs=(P(("groups", "seq"), "tensor"), P(("groups", "seq"), None, "tensor")),
        check_vma=False,
    )
```

profile of v0, /device:TPU:0, one launch (start us, length us, event | category | flops | bytes accessed | tf_op | source)
XLA Modules:
  0.0 200.9 jit_solution(16508769630650685992)
XLA Ops:
  0.6 0.0 copy-start
  0.7 0.3 iota_compare_fusion
  0.9 1.2 pad_maximum_fusion
  2.2 0.7 copy.124
  2.8 17.6 %all_gather.3 = bf16[128,2048]{1,0:T(8,128)(2,1)S(1)} all-gather(bf16[32,2048]{1,0:T(8,128)(2,1)} %param.17), channel_id=1, replica_groups=mesh['groups'=2,'seq'=4,'tensor'=4] {'seq'}, dimensions={0}, use_global_device_ids=true | all-gather | bytes 655360 | tf_op jit(solution)/shard_map/all_gather | solution.py:91
  20.4 0.3 copy.125
  20.7 2.0 %fusion.1 = (f32[2,8,128]{2,1,0:T(8,128)S(1)}, f32[2,1568,128,8]{2,1,3,0:T(8,128)S(1)}) fusion(pred[128,1568]{0,1:T(8,128)(4,1)S(1)} %iota_compare_fusion, bf16[1568,2,128,1]{0,2,3,1:T(8,128)(2,1)S(1)} %bitcast.128, bf16[128,2,8,128]{0,3,2,1:T(8,128)(2,1)S(1)} %bitcast.129), kind=kOutput, calls=%fused_computation.5 | convolution fusion | flops 831715328 | bytes 14381056 | tf_op jit(solution)/shard_map/while/body/eval_jaxpr/etkgd,epkd->ekgtp/dot_general | solution.py:31
  22.8 3.0 %fusion.2 = f32[2,8,128]{2,1,0:T(8,128)S(1)} fusion(f32[2,1568,128,8]{2,1,3,0:T(8,128)S(1)} %get-tuple-element.36, f32[2,8,128]{2,1,0:T(8,128)S(1)} %get-tuple-element.35, pred[128,1568]{0,1:T(8,128)(4,1)S(1)} %iota_compare_fusion), kind=kLoop, calls=%fused_computation.6 | loop fusion | flops 16054272 | bytes 13062144 | tf_op jit(solution)/shard_map/while/body/eval_jaxpr/reduce_sum | solution.py:38
  25.8 1.5 copy-done.1
  27.4 0.1 all_to_all.21
  27.4 0.7 reshape.433
  28.1 5.4 %all-to-all-start.2 = ((f32[4,1,512]{2,1,0:T(1,128)}), f32[4,1,512]{2,1,0:T(1,128)S(1)}, u32[]{:S(2)}, u32[]{:S(2)}) async-start(f32[4,1,512]{2,1,0:T(1,128)} %reshape.433), calls=%async_computation.2 | async-start | bytes 16384 | tf_op jit(solution)/shard_map/all_to_all | solution.py:116
  33.5 0.1 pad_maximum_fusion.1
  33.6 0.1 all_to_all.18
  33.7 0.7 reshape.431
  34.4 0.7 copy.130
  35.0 4.1 %all-to-all-done.2 = f32[4,1,512]{2,1,0:T(1,128)S(1)} async-done(((f32[4,1,512]{2,1,0:T(1,128)}), f32[4,1,512]{2,1,0:T(1,128)S(1)}, u32[]{:S(2)}, u32[]{:S(2)}) %all-to-all-start.2) | async-done | bytes 8224 | tf_op jit(solution)/shard_map/all_to_all | solution.py:116
  39.1 3.2 %all-to-all-start = ((f32[4,1,512]{2,1,0:T(1,128)}), f32[4,1,512]{2,1,0:T(1,128)S(1)}, u32[]{:S(2)}, u32[]{:S(2)}) async-start(f32[4,1,512]{2,1,0:T(1,128)} %reshape.431), calls=%async_computation | async-start | bytes 16384 | tf_op jit(solution)/shard_map/all_to_all | solution.py:115
  42.4 6.5 %fusion.5 = f32[2,128,8,128]{3,1,2,0:T(8,128)S(1)} fusion(bf16[1568,2,128,1]{0,2,3,1:T(8,128)(2,1)S(1)} %bitcast.131, f32[2,1568,128,8]{2,1,3,0:T(8,128)} %copy-done.1, f32[2,8,128]{2,1,0:T(8,128)S(1)} %get-tuple-element.35, pred[128,1568]{0,1:T(8,128)(4,1)S(1)} %iota_compare_fusion), kind=kOutput, calls=%fused_computation.9 | convolution fusion | flops 838139904 | bytes 14905344 | tf_op jit(solution)/shard_map/while/body/eval_jaxpr/ekgtp,epkd->etkgd/dot_general | solution.py:39
  48.9 1.4 copy.132
  50.3 5.0 %all-to-all-start.1 = ((f32[128,16,128]{2,1,0:T(8,128)}), f32[128,16,128]{2,1,0:T(8,128)S(1)}, u32[]{:S(2)}, u32[]{:S(2)}) async-start(f32[128,16,128]{2,1,0:T(8,128)} %copy.132), calls=%async_computation.1 | async-start | bytes 2097152 | tf_op jit(solution)/shard_map/all_to_all | solution.py:114
  55.3 0.1 iota_compare_fusion.4
  55.4 0.4 select_reduce_fusion
  55.7 0.1 reshape.403
  55.8 0.2 reduce_window_sum.11
  56.1 0.1 select_reduce_fusion.1
  56.2 0.1 reshape.404
  56.3 12.3 %gather_fusion = bf16[32,128,2,256]{3,2,1,0:T(2,128)(2,1)} fusion(bf16[32,128,2,256]{3,2,1,0:T(2,128)(2,1)} %param.22, s32[1024]{0:T(1024)S(1)} %pad_clamp_fusion.1), kind=kCustom, calls=%fused_computation | custom fusion | bytes 8388736 | tf_op jit(solution)/shard_map/gather | solution.py:144
  68.7 7.4 %all-to-all-done.1 = f32[128,16,128]{2,1,0:T(8,128)S(1)} async-done(((f32[128,16,128]{2,1,0:T(8,128)}), f32[128,16,128]{2,1,0:T(8,128)S(1)}, u32[]{:S(2)}, u32[]{:S(2)}) %all-to-all-start.1) | async-done | bytes 1048608 | tf_op jit(solution)/shard_map/all_to_all | solution.py:114
  76.0 5.0 %all-to-all-start.3 = ((bf16[32,128,2,256]{3,2,1,0:T(2,128)(2,1)}), bf16[32,128,2,256]{3,2,1,0:T(2,128)(2,1)}, u32[]{:S(2)}, u32[]{:S(2)}) async-start(bf16[32,128,2,256]{3,2,1,0:T(2,128)(2,1)} %gather_fusion), calls=%async_computation.3 | async-start | bytes 8388608 | tf_op jit(solution)/shard_map/all_to_all | solution.py:171
  81.1 0.1 dynamic_slice.17
  81.2 0.2 fusion.49
  81.4 5.8 %psum.7 = bf16[16,128]{1,0:T(8,128)(2,1)S(1)} all-reduce(f32[16,128]{1,0:T(8,128)S(1)} %fusion.49), channel_id=1, replica_groups=mesh['groups'=2,'seq'=4,'tensor'=4] {'tensor'}, use_global_device_ids=true, to_apply=%region_12.13 | all-reduce | flops 2048 | bytes 12288 | tf_op jit(solution)/shard_map/psum | solution.py:155
  87.2 0.2 select_reduce_fusion.4
  87.4 0.1 compare_and_fusion
  87.4 0.2 fusion.28
  87.8 0.2 select_reduce_fusion.2
  88.0 0.1 dynamic_slice.16
  88.1 0.2 convert_reduce_fusion
  88.3 0.1 iota_compare_fusion.1
  88.4 0.5 broadcast.338
  88.9 0.7 reduce.4
  89.6 0.1 reshape.434
  89.7 0.7 reduce.3
  90.4 0.1 reshape.432
  90.5 0.1 copy.129
  90.6 0.1 copy.135
  90.6 0.3 multiply_reduce_fusion
  91.0 0.1 divide_convert_fusion
  91.1 0.7 copy.168
  91.8 78.9 %all-to-all-done.3 = bf16[32,128,2,256]{3,2,1,0:T(2,128)(2,1)} async-done(((bf16[32,128,2,256]{3,2,1,0:T(2,128)(2,1)}), bf16[32,128,2,256]{3,2,1,0:T(2,128)(2,1)}, u32[]{:S(2)}, u32[]{:S(2)}) %all-to-all-start.3) | async-done | bytes 4194336 | tf_op jit(solution)/shard_map/all_to_all | solution.py:171
  170.8 5.0 %copy.136 = bf16[32,128,2,256]{3,1,2,0:T(8,128)(2,1)} copy(bf16[32,128,2,256]{3,2,1,0:T(2,128)(2,1)} %all-to-all-done.3) | data formatting | bytes 8388608 | tf_op jit(solution)/shard_map/all_to_all | solution.py:171
  175.8 4.9 %gather_fusion.1 = bf16[32,128,2,256]{3,1,2,0:T(8,128)(2,1)} fusion(bf16[32,128,2,256]{3,1,2,0:T(8,128)(2,1)} %copy.136, s32[1024]{0:T(1024)S(1)} %pad_clamp_fusion), kind=kCustom, calls=%fused_computation.1 | custom fusion | bytes 8388736 | tf_op jit(solution)/shard_map/gather | solution.py:172
  180.7 2.5 %copy.137 = bf16[32,128,2,256]{3,1,0,2:T(8,128)(2,1)S(1)} copy(bf16[32,128,2,256]{3,1,2,0:T(8,128)(2,1)} %gather_fusion.1) | data formatting | bytes 8388608 | tf_op jit(solution)/shard_map/gather | solution.py:172
  183.2 2.3 %fusion.45 = (bf16[4,1024,1,256]{3,1,0,2:T(8,128)(2,1)}, bf16[4,1024,1,256]{3,1,0,2:T(8,128)(2,1)}) fusion(bf16[4,1024,2,256]{3,1,0,2:T(8,128)(2,1)S(1)} %bitcast.124), kind=kLoop, calls=%fused_computation.94 | loop fusion | bytes 8388608 | tf_op jit(solution)/shard_map/slice | solution.py:173
  185.5 3.0 %copy.140 = bf16[4,1024,1,256]{1,3,0,2:T(8,128)(2,1)S(1)} copy(bf16[4,1024,1,256]{3,1,0,2:T(8,128)(2,1)} %get-tuple-element.33) | data formatting | bytes 4194304 | tf_op jit(solution)/shard_map/slice | solution.py:173
  188.4 2.6 %copy.141 = bf16[4,1024,2,128]{3,1,2,0:T(8,128)(2,1)} copy(bf16[4,1024,2,128]{1,3,2,0:T(8,128)(2,1)S(1)} %bitcast.125) | data formatting | bytes 4194304 | tf_op jit(solution)/shard_map/concatenate | solution.py:173
  191.0 3.0 %copy.138 = bf16[4,1024,1,256]{1,3,0,2:T(8,128)(2,1)S(1)} copy(bf16[4,1024,1,256]{3,1,0,2:T(8,128)(2,1)} %get-tuple-element.34) | data formatting | bytes 4194304 | tf_op jit(solution)/shard_map/slice | solution.py:174
  194.0 2.6 %copy.139 = bf16[4,1024,2,128]{3,1,2,0:T(8,128)(2,1)} copy(bf16[4,1024,2,128]{1,3,2,0:T(8,128)(2,1)S(1)} %bitcast.126) | data formatting | bytes 4194304 | tf_op jit(solution)/shard_map/concatenate | solution.py:174
  196.6 2.7 %fusion.46 = (f32[4,2,8,4]{2,3,1,0:T(4,128)S(1)}, bf16[4,2,8,4,1028]{4,2,3,1,0:T(8,128)(2,1)S(1)}) fusion(bf16[4,4,2,128]{3,1,2,0:T(4,128)(2,1)S(1)} %bitcast.140, bf16[4,1024,2,128]{3,1,2,0:T(8,128)(2,1)} %copy.141, pred[4,4,1028]{2,1,0:T(4,128)(4,1)S(1)} %pad_add_fusion, bf16[4,4,2,8,128]{4,3,2,1,0:T(8,128)(2,1)S(1)} %reshape.409), kind=kOutput, calls=%fused_computation.95 | convolution fusion | flops 73161728 | bytes 2714688 | tf_op jit(solution)/shard_map/sub | solution.py:37
  199.4 0.5 fusion.18
  199.9 0.1 div.51
  200.0 0.1 div.52
  200.2 0.7 divide_convert_fusion.1
  (55 shorter events, 0.5 us)
Async XLA Ops:
  0.6 86.8 %copy-start = (bf16[128,2048]{1,0:T(8,128)(2,1)S(1)}, bf16[128,2048]{1,0:T(8,128)(2,1)}, u32[]{:S(2)}) copy-start(bf16[128,2048]{1,0:T(8,128)(2,1)} %param.28) | copy-start | bytes 1572868
  22.7 4.6 %copy-start.1 = (f32[2,1568,128,8]{2,1,3,0:T(8,128)}, f32[2,1568,128,8]{2,1,3,0:T(8,128)S(1)}, u32[]{:S(2)}) copy-start(f32[2,1568,128,8]{2,1,3,0:T(8,128)S(1)} %get-tuple-element.36) | copy-start | bytes 38535172
  22.8 10.8 %copy-start.3 = (bf16[1536,256]{1,0:T(8,128)(2,1)S(1)}, bf16[1536,256]{1,0:T(8,128)(2,1)}, u32[]{:S(2)}) copy-start(bf16[1536,256]{1,0:T(8,128)(2,1)} %param.21) | copy-start | bytes 2359300
  22.8 10.8 %copy-start.7 = (bf16[32,256]{1,0:T(8,128)(2,1)S(1)}, bf16[32,256]{1,0:T(8,128)(2,1)}, u32[]{:S(2)}) copy-start(bf16[32,256]{1,0:T(8,128)(2,1)} %param.19) | copy-start | bytes 49156
  28.1 11.0 %all-to-all-start.2 = ((f32[4,1,512]{2,1,0:T(1,128)}), f32[4,1,512]{2,1,0:T(1,128)S(1)}, u32[]{:S(2)}, u32[]{:S(2)}) async-start(f32[4,1,512]{2,1,0:T(1,128)} %reshape.433), calls=%async_computation.2 | async-start | bytes 16384 | tf_op jit(solution)/shard_map/all_to_all | solution.py:116
  39.1 11.1 %all-to-all-start = ((f32[4,1,512]{2,1,0:T(1,128)}), f32[4,1,512]{2,1,0:T(1,128)S(1)}, u32[]{:S(2)}, u32[]{:S(2)}) async-start(f32[4,1,512]{2,1,0:T(1,128)} %reshape.431), calls=%async_computation | async-start | bytes 16384 | tf_op jit(solution)/shard_map/all_to_all | solution.py:115
  48.8 6.5 %copy-start.11 = (s32[16]{0:T(128)S(1)}, s32[16]{0:T(128)}, u32[]{:S(2)}) copy-start(s32[16]{0:T(128)} %param.29) | copy-start | bytes 196
  48.8 6.5 %copy-start.8 = (s32[16,8]{0,1:T(8,128)S(1)}, s32[16,8]{0,1:T(8,128)}, u32[]{:S(2)}) copy-start(s32[16,8]{0,1:T(8,128)} %param.30) | copy-start | bytes 1540
  50.3 25.8 %all-to-all-start.1 = ((f32[128,16,128]{2,1,0:T(8,128)}), f32[128,16,128]{2,1,0:T(8,128)S(1)}, u32[]{:S(2)}, u32[]{:S(2)}) async-start(f32[128,16,128]{2,1,0:T(8,128)} %copy.132), calls=%async_computation.1 | async-start | bytes 2097152 | tf_op jit(solution)/shard_map/all_to_all | solution.py:114
  68.6 12.5 %copy-start.5 = (bf16[4,4,2048]{2,1,0:T(4,128)(2,1)S(1)}, bf16[4,4,2048]{2,1,0:T(4,128)(2,1)}, u32[]{:S(2)}) copy-start(bf16[4,4,2048]{2,1,0:T(4,128)(2,1)} %param.26) | copy-start | bytes 196612
  68.6 12.5 %copy-start.4 = (bf16[2048,128]{1,0:T(8,128)(2,1)S(1)}, bf16[2048,128]{1,0:T(8,128)(2,1)}, u32[]{:S(2)}) copy-start(bf16[2048,128]{1,0:T(8,128)(2,1)} %param.27) | copy-start | bytes 1572868
  68.6 18.5 %copy-start.9 = (s32[16]{0:T(128)S(1)}, s32[16]{0:T(128)}, u32[]{:S(2)}) copy-start(s32[16]{0:T(128)} %param.32) | copy-start | bytes 196
  68.7 18.5 %copy-start.10 = (s32[16]{0:T(128)S(1)}, s32[16]{0:T(128)}, u32[]{:S(2)}) copy-start(s32[16]{0:T(128)} %param.33) | copy-start | bytes 196
  68.7 19.0 %copy-start.6 = (bf16[4,4,2048]{2,1,0:T(4,128)(2,1)S(1)}, bf16[4,4,2048]{2,1,0:T(4,128)(2,1)}, u32[]{:S(2)}) copy-start(bf16[4,4,2048]{2,1,0:T(4,128)(2,1)} %param.23) | copy-start | bytes 196612
  68.7 19.1 %copy-start.14 = (s32[16]{0:T(128)S(1)}, s32[16]{0:T(128)}, u32[]{:S(2)}) copy-start(s32[16]{0:T(128)} %param.31) | copy-start | bytes 196
  76.0 94.7 %all-to-all-start.3 = ((bf16[32,128,2,256]{3,2,1,0:T(2,128)(2,1)}), bf16[32,128,2,256]{3,2,1,0:T(2,128)(2,1)}, u32[]{:S(2)}, u32[]{:S(2)}) async-start(bf16[32,128,2,256]{3,2,1,0:T(2,128)(2,1)} %gather_fusion), calls=%async_computation.3 | async-start | bytes 8388608 | tf_op jit(solution)/shard_map/all_to_all | solution.py:171
  191.0 5.6 %copy-start.12 = (bf16[4,4,256]{2,1,0:T(4,128)(2,1)S(1)}, bf16[4,4,256]{2,1,0:T(4,128)(2,1)}, u32[]{:S(2)}) copy-start(bf16[4,4,256]{2,1,0:T(4,128)(2,1)} %param.24) | copy-start | bytes 24580
  196.6 2.7 %copy-start.2 = (bf16[4,1024,2,128]{3,1,2,0:T(8,128)(2,1)S(1)}, bf16[4,1024,2,128]{3,1,2,0:T(8,128)(2,1)}, u32[]{:S(2)}) copy-start(bf16[4,1024,2,128]{3,1,2,0:T(8,128)(2,1)} %copy.139) | copy-start | bytes 6291460
  196.6 2.7 %copy-start.13 = (bf16[4,4,256]{2,1,0:T(4,128)(2,1)S(1)}, bf16[4,4,256]{2,1,0:T(4,128)(2,1)}, u32[]{:S(2)}) copy-start(bf16[4,4,256]{2,1,0:T(4,128)(2,1)} %param.25) | copy-start | bytes 24580
where the time goes:
time: 202 us; the launch traced here: 201 us
  waiting for transfers between devices  90.4 us (45%)
  local copies, waits for them, and re-layouts  46.6 us (23%)
  blocking collectives  23.3 us (12%)
  starting transfers between devices  18.7 us (9%)
  matrix products  12.1 us (6%)
  other arithmetic  8.73 us (4%)
    all_to_all x1, waiting for transfers between devices, per_device(): lax.all_to_all(outgoing, 'seq', split_axis=0, concat_axis=0, tiled=True)  78.9 us
    all_gather x1, blocking collectives, per_device(): everyone = lax.all_gather(final_block_queries, 'seq', axis=0, tiled=True)  17.6 us
    gather x1, local copies, waits for them, and re-layouts, per_device(): outgoing = paged_cache_pool[send_place]  12.3 us
    gather x2, local copies, waits for them, and re-layouts, per_device(): incoming[arrive].reshape(slots_here, page_count * page_len, 2, -1)  7.38 us
    all_to_all x1, waiting for transfers between devices, per_device(): lax.all_to_all(summed, 'seq', split_axis=0, concat_axis=0, tiled=True)  7.36 us
    dot_general x2, matrix products, partial_softmax(): jnp.einsum('ekgtp,epkd->etkgd', weights.astype(jnp.bfloat16), value_head_...  6.91 us
    psum x1, blocking collectives, per_device(): lax.psum(jnp.dot(hidden_input_rows, adapter_down_maps, preferred_element_...  5.75 us
    all_to_all x1, starting transfers between devices, per_device(): lax.all_to_all(row_total, 'seq', split_axis=0, concat_axis=0, tiled=True)  5.39 us
  transfers between devices with their start and end apart: 4, of which 3 were waited for; matrix products, arithmetic and copies ran while one was open for 14% of the time, Pallas kernels for 0%

commit v1 on v0

--- a/solution.py
+++ b/solution.py
@@ -6,6 +6,40 @@
 HEAD_SIZE = 128
 LARGEST_RANK = 16
 MASKED = -1e30
+
+
+def refer_positions(panel, dim_k, content):
+    side_arr = panel.shape
+    t_next = panel.reshape(
+        *side_arr[:dim_k], content, side_arr[dim_k] // content, *side_arr[dim_k + 1 :]
+    )
+    tall = jnp.moveaxis(t_next, dim_k, 0)
+    return tall
+
+
+def list_patches_over_axis(tile_in, dim_no):
+    tile_in = jnp.moveaxis(tile_in, 0, dim_no)
+    block_last = tile_in.shape
+    plain = tile_in.reshape(
+        *block_last[:dim_no], block_last[dim_no] * block_last[dim_no + 1], *block_last[dim_no + 2 :]
+    )
+    return plain
+
+
+def derive_tables(inner_x, axis_id, sheet, vals=0):
+    w1, parts_out = (lax.axis_size(axis_id), lax.axis_index(axis_id))
+    y = refer_positions(inner_x, sheet, w1)
+    so_far_all = [y[parts_out]]
+    u = 1
+    while u < w1:
+        vec_out = y[(parts_out + u) % w1]
+        so_far_all.append(
+            lax.ppermute(vec_out, axis_id, [(hop_no, (hop_no + u) % w1) for hop_no in range(w1)])
+        )
+        u = u + 1
+    y = jnp.stack(so_far_all)[(parts_out - jnp.arange(w1)) % w1]
+    r1 = list_patches_over_axis(y, vals)
+    return r1
 
 
 def lookup_rows(lookup, positions):
@@ -168,7 +202,7 @@
     query_vectors = (step_slot_queries.astype(jnp.float32) + raised_queries).astype(jnp.bfloat16)
     step_pos = jnp.arange(decode_step_count, dtype=jnp.int32)
     fresh_ok = step_pos[None, :] <= step_pos[:, None]
-    incoming = lax.all_to_all(outgoing, "seq", split_axis=0, concat_axis=0, tiled=True)
+    incoming = derive_tables(outgoing, "seq", 0)
     gathered_pages = incoming[arrive].reshape(slots_here, page_count * page_len, 2, -1)
     all_keys = jnp.concatenate([gathered_pages[:, :, 0], step_token_keys], axis=1)
     all_values = jnp.concatenate([gathered_pages[:, :, 1], step_token_values], axis=1)

time: 202 us -> 216 us (1.069)
  waiting for transfers between devices: 90.4 us -> 2.89 us
  blocking collectives: 23.3 us -> 103 us
  local copies, waits for them, and re-layouts: 46.6 us -> 58.2 us
  other arithmetic: 8.73 us -> 14.7 us
    all_gather x1, blocking collectives: 17.6 us -> 97.2 us  [per_device(): everyone = lax.all_gather(final_block_queries, 'seq', axis=0, tiled=True)]
    all_to_all x1 -> x0, waiting for transfers between devices: 78.9 us -> none  [per_device(): lax.all_to_all(outgoing, 'seq', split_axis=0, concat_axis=0, tiled=True)]
    all_to_all x1, waiting for transfers between devices: 7.36 us -> 0.01 us  [per_device(): lax.all_to_all(summed, 'seq', split_axis=0, concat_axis=0, tiled=True)]
    ppermute x0 -> x3, starting transfers between devices: none -> 6.99 us  [derive_tables(): lax.ppermute(vec_out, axis_id, [(hop_no, (hop_no + u) % w1) for hop_no in...]
    all_to_all x1 -> x0, starting transfers between devices: 5.04 us -> none  [per_device(): lax.all_to_all(outgoing, 'seq', split_axis=0, concat_axis=0, tiled=True)]
    all_to_all x1 -> x0, local copies, waits for them, and re-layouts: 5.02 us -> none  [per_device(): lax.all_to_all(outgoing, 'seq', split_axis=0, concat_axis=0, tiled=True)]
    gather x1 -> x2, local copies, waits for them, and re-layouts: 12.3 us -> 17.3 us  [per_device(): outgoing = paged_cache_pool[send_place]]
    gather x0 -> x1, local copies, waits for them, and re-layouts: none -> 4.97 us  [derive_tables(): y = jnp.stack(so_far_all)[(parts_out - jnp.arange(w1)) % w1]]
  transfers between devices with their start and end apart: 4 -> 6, of which waited for: 3 -> 1; matrix products, arithmetic and copies ran while one was open for 14% -> 27% of each run, Pallas kernels for 0% -> 0%
where the time goes in v1:
time: 216 us; the launch traced here: 215 us
  blocking collectives  103 us (48%)
  local copies, waits for them, and re-layouts  58.2 us (27%)
  starting transfers between devices  20.4 us (9%)
  other arithmetic  14.7 us (7%)
  matrix products  14.1 us (7%)
  waiting for transfers between devices  2.89 us (1%)
    all_gather x1, blocking collectives, per_device(): everyone = lax.all_gather(final_block_queries, 'seq', axis=0, tiled=True)  97.2 us
    gather x2, local copies, waits for them, and re-layouts, per_device(): outgoing = paged_cache_pool[send_place]  17.3 us
    dot_general x2, matrix products, partial_softmax(): jnp.einsum('ekgtp,epkd->etkgd', weights.astype(jnp.bfloat16), value_head_...  8.22 us
    gather x2, local copies, waits for them, and re-layouts, per_device(): incoming[arrive].reshape(slots_here, page_count * page_len, 2, -1)  7.38 us
    ppermute x3, starting transfers between devices, derive_tables(): lax.ppermute(vec_out, axis_id, [(hop_no, (hop_no + u) % w1) for hop_no in...  6.99 us
    psum x1, blocking collectives, per_device(): lax.psum(jnp.dot(hidden_input_rows, adapter_down_maps, preferred_element_...  6.02 us
    slice x2, local copies, waits for them, and re-layouts, per_device(): gathered_pages[:, :, 0]  5.2 us
    all_to_all x1, starting transfers between devices, per_device(): lax.all_to_all(row_max, 'seq', split_axis=0, concat_axis=0, tiled=True)  5 us
  transfers between devices with their start and end apart: 6, of which 1 were waited for; matrix products, arithmetic and copies ran while one was open for 27% of the time, Pallas kernels for 0%

profile of v1, /device:TPU:0, one launch (start us, length us, event | category | flops | bytes accessed | tf_op | source)
XLA Modules:
  0.0 214.7 jit_solution(10870751230352460628)
XLA Ops:
  0.7 0.8 iota_compare_fusion.4
  1.5 1.0 select_reduce_fusion
  2.5 0.1 reshape.458
  2.6 0.2 reduce_window_sum.11
  2.8 0.1 select_reduce_fusion.1
  3.0 0.1 reshape.459
  3.1 12.3 %gather_fusion = bf16[32,128,2,256]{3,2,1,0:T(2,128)(2,1)} fusion(bf16[32,128,2,256]{3,2,1,0:T(2,128)(2,1)} %param.22, s32[1024]{0:T(1024)S(1)} %pad_clamp_fusion.2), kind=kCustom, calls=%fused_computation | custom fusion | bytes 8388736 | tf_op jit(solution)/shard_map/gather | solution.py:178
  15.4 5.0 %copy.136 = bf16[32,128,2,256]{3,1,2,0:T(8,128)(2,1)} copy(bf16[32,128,2,256]{3,2,1,0:T(2,128)(2,1)} %gather_fusion) | data formatting | bytes 8388608 | tf_op jit(solution)/shard_map/gather | solution.py:178
  20.4 4.0 %constant_dynamic-slice_fusion.1 = (bf16[1,8,128,2,256]{4,2,3,1,0:T(8,128)(2,1)S(1)}, bf16[8,128,2,256]{3,1,2,0:T(8,128)(2,1)}, bf16[8,128,2,256]{3,1,2,0:T(8,128)(2,1)}, bf16[8,128,2,256]{3,1,2,0:T(8,128)(2,1)}) fusion(bf16[4,8,128,2,256]{4,2,3,1,0:T(8,128)(2,1)} %bitcast.137, s32[]{:T(128)S(6)} %select_n.177, s32[]{:T(128)S(6)} %select_n.183, ...), kind=kLoop, calls=%fused_computation.84 | loop fusion | bytes 8388624 | tf_op jit(solution)/shard_map/dynamic_slice | solution.py:32
  24.4 3.1 %collective-permute-start = (bf16[8,128,2,256]{3,1,2,0:T(8,128)(2,1)}, bf16[8,128,2,256]{3,1,2,0:T(8,128)(2,1)}, u32[]{:S(2)}, u32[]{:S(2)}) collective-permute-start(bf16[8,128,2,256]{3,1,2,0:T(8,128)(2,1)} %get-tuple-element.38), channel_id=1, source_target_pairs={{0,4},{4,8},{8,12},{12,0},{1,5},{5,9},{9,13},{13,1},{2,6},{6,10},{... | collective-permute-start | bytes 3145736 | tf_op jit(solution)/shard_map/ppermute | solution.py:37
  27.5 2.6 %collective-permute-start.1 = (bf16[8,128,2,256]{3,1,2,0:T(8,128)(2,1)}, bf16[8,128,2,256]{3,1,2,0:T(8,128)(2,1)}, u32[]{:S(2)}, u32[]{:S(2)}) collective-permute-start(bf16[8,128,2,256]{3,1,2,0:T(8,128)(2,1)} %get-tuple-element.37), channel_id=1, source_target_pairs={{0,8},{4,12},{8,0},{12,4},{1,9},{5,13},{9,1},{13,5},{2,10},{6,14},... | collective-permute-start | bytes 3145736 | tf_op jit(solution)/shard_map/ppermute | solution.py:37
  30.1 1.3 collective-permute-start.2
  31.4 0.3 iota_compare_fusion
  31.7 0.9 pad_maximum_fusion.1
  32.7 1.5 copy.124
  34.2 97.2 %all_gather.3 = bf16[128,2048]{1,0:T(8,128)(2,1)} all-gather(bf16[32,2048]{1,0:T(8,128)(2,1)S(1)} %copy-done.7), channel_id=1, replica_groups=mesh['groups'=2,'seq'=4,'tensor'=4] {'seq'}, dimensions={0}, use_global_device_ids=true | all-gather | bytes 655360 | tf_op jit(solution)/shard_map/all_gather | solution.py:125
  131.4 1.3 copy.125
  132.7 2.0 fusion.1
  134.8 3.0 %fusion.2 = f32[2,8,128]{2,1,0:T(8,128)S(1)} fusion(f32[2,1568,128,8]{2,1,3,0:T(8,128)S(1)} %get-tuple-element.40, f32[2,8,128]{2,1,0:T(8,128)S(1)} %get-tuple-element.39, pred[128,1568]{0,1:T(8,128)(4,1)S(1)} %iota_compare_fusion), kind=kLoop, calls=%fused_computation.7 | loop fusion | flops 16054272 | bytes 13062144 | tf_op jit(solution)/shard_map/while/body/eval_jaxpr/reduce_sum | solution.py:72
  137.9 1.7 copy-done.2
  139.6 0.1 all_to_all.18
  139.7 0.7 reshape.498
  140.3 4.2 %all-to-all-start.2 = ((f32[4,1,512]{2,1,0:T(1,128)}), f32[4,1,512]{2,1,0:T(1,128)S(1)}, u32[]{:S(2)}, u32[]{:S(2)}) async-start(f32[4,1,512]{2,1,0:T(1,128)} %reshape.498), calls=%async_computation.2 | async-start | bytes 16384 | tf_op jit(solution)/shard_map/all_to_all | solution.py:150
  144.5 0.2 convert_reduce_fusion
  144.7 0.1 dynamic_slice.33
  144.9 0.2 fusion.51
  145.0 6.0 %psum.7 = bf16[16,128]{1,0:T(8,128)(2,1)S(1)} all-reduce(f32[16,128]{1,0:T(8,128)S(1)} %fusion.51), channel_id=1, replica_groups=mesh['groups'=2,'seq'=4,'tensor'=4] {'tensor'}, use_global_device_ids=true, to_apply=%region_12.13 | all-reduce | flops 2048 | bytes 12288 | tf_op jit(solution)/shard_map/psum | solution.py:189
  151.1 0.2 select_reduce_fusion.2
  151.3 0.1 dynamic_slice.32
  151.3 0.1 iota_compare_fusion.1
  151.5 1.4 copy.130
  152.9 6.7 %fusion.5 = f32[2,128,8,128]{3,1,2,0:T(8,128)S(1)} fusion(bf16[1568,2,128,1]{0,2,3,1:T(8,128)(2,1)} %bitcast.145, f32[2,1568,128,8]{2,1,3,0:T(8,128)} %copy-done.2, f32[2,8,128]{2,1,0:T(8,128)S(1)} %get-tuple-element.39, pred[128,1568]{0,1:T(8,128)(4,1)S(1)} %iota_compare_fusion), kind=kOutput, calls=%fused_computation.10 | convolution fusion | flops 838139904 | bytes 14905344 | tf_op jit(solution)/shard_map/while/body/eval_jaxpr/ekgtp,epkd->etkgd/dot_general | solution.py:73
  159.7 0.2 select_reduce_fusion.4
  159.9 0.1 compare_and_fusion
  160.0 0.2 fusion.28
  160.3 0.1 all_to_all.15
  160.4 0.7 reshape.496
  161.1 5.0 %all-to-all-start = ((f32[4,1,512]{2,1,0:T(1,128)}), f32[4,1,512]{2,1,0:T(1,128)S(1)}, u32[]{:S(2)}, u32[]{:S(2)}) async-start(f32[4,1,512]{2,1,0:T(1,128)} %reshape.496), calls=%async_computation | async-start | bytes 16384 | tf_op jit(solution)/shard_map/all_to_all | solution.py:149
  166.1 1.4 copy.132
  167.5 0.5 broadcast.410
  168.0 0.7 reduce.4
  168.7 0.1 reshape.499
  168.8 2.9 %all-to-all-done = f32[4,1,512]{2,1,0:T(1,128)S(1)} async-done(((f32[4,1,512]{2,1,0:T(1,128)}), f32[4,1,512]{2,1,0:T(1,128)S(1)}, u32[]{:S(2)}, u32[]{:S(2)}) %all-to-all-start) | async-done | bytes 8224 | tf_op jit(solution)/shard_map/all_to_all | solution.py:149
  171.7 4.3 %all-to-all-start.1 = ((f32[128,16,128]{2,1,0:T(8,128)}), f32[128,16,128]{2,1,0:T(8,128)}, u32[]{:S(2)}, u32[]{:S(2)}) async-start(f32[128,16,128]{2,1,0:T(8,128)} %copy.132), calls=%async_computation.1 | async-start | bytes 2097152 | tf_op jit(solution)/shard_map/all_to_all | solution.py:148
  175.9 0.7 reduce.3
  176.6 0.1 reshape.497
  176.7 0.1 copy.129
  176.9 3.6 %pad_maximum_fusion = bf16[4,8,128,2,256]{4,2,3,1,0:T(8,128)(2,1)} fusion(bf16[1,8,128,2,256]{4,2,3,1,0:T(8,128)(2,1)} %bitcast.23, bf16[1,8,128,2,256]{4,2,3,1,0:T(8,128)(2,1)} %bitcast.21, bf16[1,8,128,2,256]{4,2,3,1,0:T(8,128)(2,1)} %bitcast.19, bf16[1,8,128,2,256]{4,2,3,1,0:T(8,128)(2,1)S(1)} %get-tuple-element.35), kind=kLoop, calls=%fused_computation.12 | loop fusion | flops 6291456 | bytes 8388608 | tf_op jit(solution)/shard_map/stack | solution.py:40
  180.5 5.0 %gather_fusion.1 = bf16[4,8,128,2,256]{4,2,3,1,0:T(8,128)(2,1)} fusion(bf16[4,8,128,2,256]{4,2,3,1,0:T(8,128)(2,1)} %pad_maximum_fusion, s32[1024]{0:T(1024)S(1)} %pad_clamp_fusion.1), kind=kCustom, calls=%fused_computation.1 | custom fusion | bytes 8388624 | tf_op jit(solution)/shard_map/gather | solution.py:40
  185.4 4.9 %gather_fusion.2 = bf16[32,128,2,256]{3,1,2,0:T(8,128)(2,1)} fusion(bf16[32,128,2,256]{3,1,2,0:T(8,128)(2,1)} %bitcast.138, s32[1024]{0:T(1024)S(1)} %pad_clamp_fusion), kind=kCustom, calls=%fused_computation.2 | custom fusion | bytes 8388736 | tf_op jit(solution)/shard_map/gather | solution.py:206
  190.4 2.5 %copy.137 = bf16[32,128,2,256]{3,1,0,2:T(8,128)(2,1)S(1)} copy(bf16[32,128,2,256]{3,1,2,0:T(8,128)(2,1)} %gather_fusion.2) | data formatting | bytes 8388608 | tf_op jit(solution)/shard_map/gather | solution.py:206
  192.8 2.2 %fusion.47 = (bf16[4,1024,1,256]{3,1,0,2:T(8,128)(2,1)}, bf16[4,1024,1,256]{3,1,0,2:T(8,128)(2,1)}) fusion(bf16[4,1024,2,256]{3,1,0,2:T(8,128)(2,1)S(1)} %bitcast.139), kind=kLoop, calls=%fused_computation.107 | loop fusion | bytes 8388608 | tf_op jit(solution)/shard_map/slice | solution.py:207
  195.0 3.0 %copy.140 = bf16[4,1024,1,256]{1,3,0,2:T(8,128)(2,1)S(1)} copy(bf16[4,1024,1,256]{3,1,0,2:T(8,128)(2,1)} %get-tuple-element.33) | data formatting | bytes 4194304 | tf_op jit(solution)/shard_map/slice | solution.py:207
  198.0 2.6 %copy.141 = bf16[4,1024,2,128]{3,1,2,0:T(8,128)(2,1)} copy(bf16[4,1024,2,128]{1,3,2,0:T(8,128)(2,1)S(1)} %bitcast.140) | data formatting | bytes 4194304 | tf_op jit(solution)/shard_map/concatenate | solution.py:207
  200.6 3.0 %copy.138 = bf16[4,1024,1,256]{1,3,0,2:T(8,128)(2,1)S(1)} copy(bf16[4,1024,1,256]{3,1,0,2:T(8,128)(2,1)} %get-tuple-element.34) | data formatting | bytes 4194304 | tf_op jit(solution)/shard_map/slice | solution.py:208
  203.6 2.6 %copy.139 = bf16[4,1024,2,128]{3,1,2,0:T(8,128)(2,1)} copy(bf16[4,1024,2,128]{1,3,2,0:T(8,128)(2,1)S(1)} %bitcast.141) | data formatting | bytes 4194304 | tf_op jit(solution)/shard_map/concatenate | solution.py:208
  206.2 3.5 %fusion.48 = (f32[4,2,8,4]{2,3,1,0:T(4,128)S(1)}, bf16[4,2,8,4,1028]{4,2,3,1,0:T(8,128)(2,1)}) fusion(bf16[4,4,2,128]{3,1,2,0:T(4,128)(2,1)S(1)} %bitcast.154, bf16[4,1024,2,128]{3,1,2,0:T(8,128)(2,1)} %copy.141, pred[4,4,1028]{2,1,0:T(4,128)(4,1)S(1)} %pad_add_fusion, bf16[4,4,2,8,128]{4,3,2,1,0:T(8,128)(2,1)S(1)} %reshape.466), kind=kOutput, calls=%fused_computation.108 | convolution fusion | flops 73161728 | bytes 2714688 | tf_op jit(solution)/shard_map/sub | solution.py:71
  209.7 1.5 fusion.18
  211.3 0.1 div.51
  211.4 0.1 div.52
  211.6 0.7 divide_convert_fusion.1
  212.3 1.6 multiply_reduce_fusion
  213.8 0.1 divide_convert_fusion
  214.0 0.7 copy.168
  (70 shorter events, 0.7 us)
Async XLA Ops:
  0.6 159.3 %copy-start = (bf16[128,2048]{1,0:T(8,128)(2,1)S(1)}, bf16[128,2048]{1,0:T(8,128)(2,1)}, u32[]{:S(2)}) copy-start(bf16[128,2048]{1,0:T(8,128)(2,1)} %param.28) | copy-start | bytes 1572868
  20.4 11.3 %copy-start.4 = (bf16[1536,256]{1,0:T(8,128)(2,1)S(1)}, bf16[1536,256]{1,0:T(8,128)(2,1)}, u32[]{:S(2)}) copy-start(bf16[1536,256]{1,0:T(8,128)(2,1)} %param.20) | copy-start | bytes 2359300
  20.4 11.3 %copy-start.10 = (bf16[32,256]{1,0:T(8,128)(2,1)S(1)}, bf16[32,256]{1,0:T(8,128)(2,1)}, u32[]{:S(2)}) copy-start(bf16[32,256]{1,0:T(8,128)(2,1)} %param.18) | copy-start | bytes 49156
  20.4 13.8 %copy-start.7 = (bf16[32,2048]{1,0:T(8,128)(2,1)S(1)}, bf16[32,2048]{1,0:T(8,128)(2,1)}, u32[]{:S(2)}) copy-start(bf16[32,2048]{1,0:T(8,128)(2,1)} %param.17) | copy-start | bytes 393220
  24.4 152.4 %collective-permute-start = (bf16[8,128,2,256]{3,1,2,0:T(8,128)(2,1)}, bf16[8,128,2,256]{3,1,2,0:T(8,128)(2,1)}, u32[]{:S(2)}, u32[]{:S(2)}) collective-permute-start(bf16[8,128,2,256]{3,1,2,0:T(8,128)(2,1)} %get-tuple-element.38), channel_id=1, source_target_pairs={{0,4},{4,8},{8,12},{12,0},{1,5},{5,9},{9,13},{13,1},{2,6},{6,10},{... | collective-permute-start | bytes 3145736 | tf_op jit(solution)/shard_map/ppermute | solution.py:37
  27.5 149.4 %collective-permute-start.1 = (bf16[8,128,2,256]{3,1,2,0:T(8,128)(2,1)}, bf16[8,128,2,256]{3,1,2,0:T(8,128)(2,1)}, u32[]{:S(2)}, u32[]{:S(2)}) collective-permute-start(bf16[8,128,2,256]{3,1,2,0:T(8,128)(2,1)} %get-tuple-element.37), channel_id=1, source_target_pairs={{0,8},{4,12},{8,0},{12,4},{1,9},{5,13},{9,1},{13,5},{2,10},{6,14},... | collective-permute-start | bytes 3145736 | tf_op jit(solution)/shard_map/ppermute | solution.py:37
  30.1 146.8 %collective-permute-start.2 = (bf16[8,128,2,256]{3,1,2,0:T(8,128)(2,1)}, bf16[8,128,2,256]{3,1,2,0:T(8,128)(2,1)}, u32[]{:S(2)}, u32[]{:S(2)}) collective-permute-start(bf16[8,128,2,256]{3,1,2,0:T(8,128)(2,1)} %get-tuple-element.36), channel_id=1, source_target_pairs={{0,12},{4,0},{8,4},{12,8},{1,13},{5,1},{9,5},{13,9},{2,14},{6,2},{... | collective-permute-start | bytes 3145736 | tf_op jit(solution)/shard_map/ppermute | solution.py:37
  134.8 4.8 %copy-start.2 = (f32[2,1568,128,8]{2,1,3,0:T(8,128)}, f32[2,1568,128,8]{2,1,3,0:T(8,128)S(1)}, u32[]{:S(2)}) copy-start(f32[2,1568,128,8]{2,1,3,0:T(8,128)S(1)} %get-tuple-element.40) | copy-start | bytes 38535172
  134.8 10.0 %copy-start.12 = (s32[16]{0:T(128)S(1)}, s32[16]{0:T(128)}, u32[]{:S(2)}) copy-start(s32[16]{0:T(128)} %param.29) | copy-start | bytes 196
  134.8 10.1 %copy-start.8 = (bf16[4,4,2048]{2,1,0:T(4,128)(2,1)S(1)}, bf16[4,4,2048]{2,1,0:T(4,128)(2,1)}, u32[]{:S(2)}) copy-start(bf16[4,4,2048]{2,1,0:T(4,128)(2,1)} %param.26) | copy-start | bytes 196612
  134.8 10.1 %copy-start.6 = (bf16[2048,128]{1,0:T(8,128)(2,1)S(1)}, bf16[2048,128]{1,0:T(8,128)(2,1)}, u32[]{:S(2)}) copy-start(bf16[2048,128]{1,0:T(8,128)(2,1)} %param.27) | copy-start | bytes 1572868
  134.8 16.3 %copy-start.17 = (s32[16]{0:T(128)S(1)}, s32[16]{0:T(128)}, u32[]{:S(2)}) copy-start(s32[16]{0:T(128)} %param.31) | copy-start | bytes 196
  134.8 16.6 %copy-start.5 = (bf16[1536,256]{1,0:T(8,128)(2,1)S(1)}, bf16[1536,256]{1,0:T(8,128)(2,1)}, u32[]{:S(2)}) copy-start(bf16[1536,256]{1,0:T(8,128)(2,1)} %param.21) | copy-start | bytes 2359300
  134.8 16.6 %copy-start.11 = (bf16[32,256]{1,0:T(8,128)(2,1)S(1)}, bf16[32,256]{1,0:T(8,128)(2,1)}, u32[]{:S(2)}) copy-start(bf16[32,256]{1,0:T(8,128)(2,1)} %param.19) | copy-start | bytes 49156
  140.3 20.7 %all-to-all-start.2 = ((f32[4,1,512]{2,1,0:T(1,128)}), f32[4,1,512]{2,1,0:T(1,128)S(1)}, u32[]{:S(2)}, u32[]{:S(2)}) async-start(f32[4,1,512]{2,1,0:T(1,128)} %reshape.498), calls=%async_computation.2 | async-start | bytes 16384 | tf_op jit(solution)/shard_map/all_to_all | solution.py:150
  152.9 6.8 %copy-start.13 = (s32[16]{0:T(128)S(1)}, s32[16]{0:T(128)}, u32[]{:S(2)}) copy-start(s32[16]{0:T(128)} %param.32) | copy-start | bytes 196
  152.9 6.8 %copy-start.14 = (s32[16]{0:T(128)S(1)}, s32[16]{0:T(128)}, u32[]{:S(2)}) copy-start(s32[16]{0:T(128)} %param.33) | copy-start | bytes 196
  152.9 7.3 %copy-start.9 = (bf16[4,4,2048]{2,1,0:T(4,128)(2,1)S(1)}, bf16[4,4,2048]{2,1,0:T(4,128)(2,1)}, u32[]{:S(2)}) copy-start(bf16[4,4,2048]{2,1,0:T(4,128)(2,1)} %param.23) | copy-start | bytes 196612
  161.1 10.6 %all-to-all-start = ((f32[4,1,512]{2,1,0:T(1,128)}), f32[4,1,512]{2,1,0:T(1,128)S(1)}, u32[]{:S(2)}, u32[]{:S(2)}) async-start(f32[4,1,512]{2,1,0:T(1,128)} %reshape.496), calls=%async_computation | async-start | bytes 16384 | tf_op jit(solution)/shard_map/all_to_all | solution.py:149
  171.7 40.6 %all-to-all-start.1 = ((f32[128,16,128]{2,1,0:T(8,128)}), f32[128,16,128]{2,1,0:T(8,128)}, u32[]{:S(2)}, u32[]{:S(2)}) async-start(f32[128,16,128]{2,1,0:T(8,128)} %copy.132), calls=%async_computation.1 | async-start | bytes 2097152 | tf_op jit(solution)/shard_map/all_to_all | solution.py:148
  200.6 5.6 %copy-start.15 = (bf16[4,4,256]{2,1,0:T(4,128)(2,1)S(1)}, bf16[4,4,256]{2,1,0:T(4,128)(2,1)}, u32[]{:S(2)}) copy-start(bf16[4,4,256]{2,1,0:T(4,128)(2,1)} %param.24) | copy-start | bytes 24580
  206.2 3.5 %copy-start.3 = (bf16[4,1024,2,128]{3,1,2,0:T(8,128)(2,1)S(1)}, bf16[4,1024,2,128]{3,1,2,0:T(8,128)(2,1)}, u32[]{:S(2)}) copy-start(bf16[4,1024,2,128]{3,1,2,0:T(8,128)(2,1)} %copy.139) | copy-start | bytes 6291460
  206.2 3.5 %copy-start.16 = (bf16[4,4,256]{2,1,0:T(4,128)(2,1)S(1)}, bf16[4,4,256]{2,1,0:T(4,128)(2,1)}, u32[]{:S(2)}) copy-start(bf16[4,4,256]{2,1,0:T(4,128)(2,1)} %param.25) | copy-start | bytes 24580
  206.2 8.5 %copy-start.1 = (bf16[128,2048]{1,0:T(8,128)(2,1)S(1)}, bf16[128,2048]{1,0:T(8,128)(2,1)}, u32[]{:S(2)}) copy-start(bf16[128,2048]{1,0:T(8,128)(2,1)} %param.28) | copy-start | bytes 1572868
